TPU v7x, 32 devices: a whole 2x2x4 slice. The times are simulated.
32 devices in a mesh: row: 8 (over z, core), col: 4 (over y, x).
Axes of the slice: x: 2, y: 2, z: 4, core: 2. Of those that a mesh axis runs over, the one named last changes fastest.
Arguments:
- velocity: float32 [3, 64, 64, 64], P(None, 'row', 'col'), may hold values from -6 to 6
Outputs:
- advanced: float32 [3, 64, 64, 64], P(None, 'row', 'col')
All inputs are finite; a program needn't handle non-finite values.
Results may differ from a plain program's by a relative error of at most 0.0003.
Values sent between devices are 32-bit elements.
A program may use at most 64 MiB of HBM per device.

v0:
```python
import functools

import jax
import jax.numpy as jnp
import ml_dtypes
import numpy as np
from jax import lax
from jax.experimental import pallas as pl
from jax.experimental.pallas import tpu as pltpu
from jax.sharding import PartitionSpec as P

MESH = pl.DeviceIdType.MESH
PAD = 8


def band_waves(points, shards, half, pad):
    top = (points - 1) // 3
    kept = np.arange(top + 1) if half else np.concatenate([np.arange(top + 1), np.arange(-top, 0)])
    each = -(-len(kept) // shards)
    pad = -(-each // pad) * pad
    table = np.full((shards * each,), points)
    table[: len(kept)] = kept
    out = np.full((shards, pad), points)
    out[:, :each] = table.reshape(shards, each)
    return out


def circle(points, waves):
    x = np.arange(points).reshape((-1,) + (1,) * waves.ndim)
    angle = ((x * waves) % points) * (2.0 * np.pi / points)
    real = (waves < points).astype(np.float64)
    return np.cos(angle) * real, np.sin(angle) * real


def halves(table):
    high = table.astype(np.float32).astype(ml_dtypes.bfloat16)
    low = (table - high.astype(np.float64)).astype(np.float32).astype(ml_dtypes.bfloat16)
    return np.stack([high, low])


def tables(points, rows, cols):
    kz = band_waves(points, cols, True, PAD)
    ky = band_waves(points, rows, False, PAD)
    kx = band_waves(points, 1, False, 16)[0]
    px, py = points // rows, points // cols
    cz, sz = circle(points, kz)
    zf = np.stack([cz, -sz], 2).transpose(1, 2, 3, 0).reshape(-1, points) / points
    weight = np.where(kz == 0, 1.0, 2.0)[None, :, None, :]
    zi = (np.stack([cz, -sz], 2) * weight).reshape(points, -1)

    def kron(spec, parts, eye, left, scale):
        made = [np.einsum(spec, part, np.eye(eye)).reshape(left, -1) * scale for part in parts]
        return np.concatenate(made, 1)

    cy = [a.reshape(cols, py, rows, PAD) for a in circle(points, ky)]
    cx = [a.reshape(rows, px, len(kx)) for a in circle(points, kx)]
    yf = kron("qyrt,xX->qxyrXt", cy, px, points * px, 1 / points)
    yi = kron("qyrt,xX->rxtqXy", cy, px, rows * px * PAD, 1.0)
    xf = kron("rxk,tT->rxtkT", cx, PAD, points * PAD, 1 / points)
    xi = kron("rxk,tT->ktrxT", cx, PAD, len(kx) * PAD, 1.0)
    lanes = len(kx) * PAD
    wx = np.broadcast_to(np.repeat(kx, PAD)[None, :], (PAD, lanes))
    wy = np.broadcast_to(np.tile(ky[:, None, None, :], (1, 1, len(kx), 1)).reshape(rows, 1, lanes), (rows, PAD, lanes))
    wz = np.broadcast_to(kz[:, :, None], (cols, PAD, lanes))
    waves = [np.ascontiguousarray(w).astype(np.float32) for w in (wx, wy, wz)]
    return [halves(t) for t in (zf, zi, yf, yi, xf, xi)] + waves


def dot(a, b, transposed=False):
    dims = (((1,), (1 if transposed else 0,)), ((), ()))
    return lax.dot_general(a, b, dims, preferred_element_type=jnp.float32)


def split(x):
    high = x.astype(jnp.bfloat16)
    return high, (x - high.astype(jnp.float32)).astype(jnp.bfloat16)


def dot_left(table, x, transposed=False):
    high, low = split(x)
    return dot(table[0], high, transposed) + (dot(table[0], low, transposed) + dot(table[1], high, transposed))


def dot_right(x, table):
    high, low = split(x)
    return dot(high, table[0]) + (dot(low, table[0]) + dot(high, table[1]))


def turn(re, im, table, sign):
    n, half = re.shape[0], table.shape[2] // 2
    out = dot_right(jnp.concatenate([re, im], 0), table)
    re_c, re_s, im_c, im_s = out[:n, :half], out[:n, half:], out[n:, :half], out[n:, half:]
    if sign > 0:
        return re_c - im_s, im_c + re_s
    return re_c + im_s, im_c - re_s


def cross(a, b):
    return [a[1] * b[2] - a[2] * b[1], a[2] * b[0] - a[0] * b[2], a[0] * b[1] - a[1] * b[0]]


def kernel(points, rows, cols, counts, v_ref, zf, zi, yf, yi, xf, xi, wx, wy, wz, out_ref, *scratch):
    row, col = lax.axis_index("row"), lax.axis_index("col")
    px, py = points // rows, points // cols
    cell, tile = px * py, 2 * px * PAD
    peers = {"row": (row, rows), "col": (col, cols)}
    exchanges = len(counts)
    sends, lands = scratch[:exchanges], scratch[exchanges : 2 * exchanges]
    send_sems, land_sems = scratch[2 * exchanges : 3 * exchanges], scratch[3 * exchanges :]

    barrier = pltpu.get_barrier_semaphore()
    for axis, (me, n) in peers.items():
        for d in range(1, n):
            pl.semaphore_signal(barrier, inc=1, device_id={axis: lax.rem(me + d, n)}, device_id_type=MESH)
    pl.semaphore_wait(barrier, rows + cols - 2)

    def swap(at, blocks):
        axis = counts[at]
        me, n = peers[axis]
        send, land = sends[at], lands[at]
        for j in range(n):
            send[j] = blocks[j]
        copies = []
        for d in range(1, n):
            to = lax.rem(me + d, n)
            copy = pltpu.make_async_remote_copy(
                src_ref=send.at[to], dst_ref=land.at[me], send_sem=send_sems[at].at[d - 1],
                recv_sem=land_sems[at].at[d - 1], device_id={axis: to}, device_id_type=MESH)
            copy.start()
            copies.append(copy)
        land[me] = send[me]
        for copy in copies:
            copy.wait()
        return [land[j] for j in range(n)]

    lane = lax.broadcasted_iota(jnp.int32, (1, tile), 1) < tile // 2
    flip = lambda a: pltpu.roll(a, tile // 2, 1)

    def weave(re, im):
        blocks = []
        for j in range(re.shape[1] // tile):
            a, b = re[:, j * tile : (j + 1) * tile], im[:, j * tile : (j + 1) * tile]
            blocks += [jnp.where(lane, a, flip(b)), jnp.where(lane, flip(a), b)]
        return blocks

    def unweave(blocks):
        re, im = [], []
        for a, b in zip(blocks[::2], blocks[1::2]):
            re.append(jnp.where(lane, a, flip(b)))
            im.append(jnp.where(lane, flip(a), b))
        return jnp.concatenate(re, 1), jnp.concatenate(im, 1)

    def spectra(at, lines):
        deep = 2 * PAD
        got = swap(at, [lines[p * deep : (p + 1) * deep] for p in range(cols)])
        pair = []
        for part in range(2):
            stacks = [
                jnp.concatenate([g[part * PAD : (part + 1) * PAD, c * cell : (c + 1) * cell] for c in range(3)], 0)
                for g in got
            ]
            pair.append(jnp.concatenate(stacks, 1))
        got = swap(at + 1, weave(*turn(*pair, yf, -1)))
        return turn(*unweave(got), xf, -1)

    def grids(at, re, im):
        n = re.shape[0] // PAD
        got = swap(at, weave(*turn(re, im, xi, 1)))
        re, im = turn(*unweave(got), yi, 1)
        got = swap(at + 1, [
            jnp.concatenate([re[:, q * cell : (q + 1) * cell], im[:, q * cell : (q + 1) * cell]], 1)
            for q in range(cols)])
        stacks = []
        for c in range(n):
            parts = [g[c * PAD : (c + 1) * PAD, p * cell : (p + 1) * cell] for g in got for p in range(2)]
            stacks.append(jnp.concatenate(parts, 0))
        return dot_left(zi, jnp.concatenate(stacks, 1))

    waves = (wx[...], wy[row], wz[col])
    kept = functools.reduce(jnp.logical_and, [3.0 * jnp.abs(w) < points for w in waves])
    squared = waves[0] * waves[0] + waves[1] * waves[1] + waves[2] * waves[2]
    safe_norm = jnp.where(squared > 0, squared, 1.0)
    viscous = squared * (1.0 / points)

    def project(b):
        b = [jnp.where(kept, b[c * PAD : (c + 1) * PAD], 0.0) for c in range(3)]
        along = (waves[0] * b[0] + waves[1] * b[1] + waves[2] * b[2]) / safe_norm
        return [b[c] - waves[c] * along for c in range(3)]

    def tendency(at, re, im):
        joined = grids(
            at,
            jnp.concatenate(re + [-w for w in cross(waves, im)], 0),
            jnp.concatenate(im + cross(waves, re), 0))
        fields = [joined[:, c * cell : (c + 1) * cell] for c in range(6)]
        product = jnp.concatenate(cross(fields[:3], fields[3:]), 1)
        b_re, b_im = spectra(at + 2, dot_left(zf, product))
        return (
            [b - viscous * a for b, a in zip(project(b_re), re)],
            [b - viscous * a for b, a in zip(project(b_im), im)],
        )

    b_re, b_im = spectra(0, dot_left(zf, v_ref[...], transposed=True))
    re, im = project(b_re), project(b_im)
    step = 2.0 / points
    r1_re, r1_im = tendency(2, re, im)
    mid_re = [a + step * r for a, r in zip(re, r1_re)]
    mid_im = [a + step * r for a, r in zip(im, r1_im)]
    r2_re, r2_im = tendency(6, mid_re, mid_im)
    end_re = [a + 0.5 * step * (r + s) for a, r, s in zip(re, r1_re, r2_re)]
    end_im = [a + 0.5 * step * (r + s) for a, r, s in zip(im, r1_im, r2_im)]
    out_ref[...] = grids(10, jnp.concatenate(end_re, 0), jnp.concatenate(end_im, 0))


def solution(mesh):
    rows, cols = mesh.shape["row"], mesh.shape["col"]

    def local(velocity):
        points = velocity.shape[3]
        px, py = points // rows, points // cols
        cell, tile = px * py, 2 * px * PAD
        consts = tables(points, rows, cols)
        forward = [(cols, 2 * PAD, 3 * cell), (rows, 3 * PAD, tile)]
        inverse = lambda n: [(rows, n * PAD, tile), (cols, n * PAD, 2 * cell)]
        shapes = forward + 2 * (inverse(6) + forward) + inverse(3)
        axes = ["col", "row"] + 2 * ["row", "col", "col", "row"] + ["row", "col"]
        sems = [pltpu.SemaphoreType.DMA(((rows if a == "row" else cols) - 1,)) for a in axes]
        buffers = [pltpu.VMEM(s, jnp.float32) for s in shapes]
        out = pl.pallas_call(
            functools.partial(kernel, points, rows, cols, axes),
            out_shape=jax.ShapeDtypeStruct((points, 3 * cell), jnp.float32),
            in_specs=[pl.BlockSpec(memory_space=pltpu.VMEM)] * (1 + len(consts)),
            out_specs=pl.BlockSpec(memory_space=pltpu.VMEM),
            scratch_shapes=buffers + buffers + sems + sems,
            compiler_params=pltpu.CompilerParams(
                collective_id=0, has_side_effects=True, vmem_limit_bytes=60 * 1024 * 1024),
        )(velocity.reshape(3 * cell, points), *[jnp.asarray(c) for c in consts])
        return out.reshape(points, 3, px, py).transpose(1, 2, 3, 0)

    placed = P(None, "row", "col", None)
    return jax.shard_map(local, mesh=mesh, in_specs=(placed,), out_specs=placed, check_vma=False)
```

profile of v0, /device:TPU:0, one launch (start us, length us, event | category | flops | bytes accessed | tf_op | source)
XLA Modules:
  0.0 72.9 jit_solution(17477620179366667589)
XLA Ops:
  0.0 71.2 %shard_map.100 = f32[64,384]{1,0:T(8,128)} custom-call(f32[384,64]{1,0:T(8,128)} %bitcast.4, bf16[2,64,64]{2,1,0:T(8,128)(2,1)} %constant.18.clone.zf, bf16[2,64,64]{2,1,0:T(8,128)(2,1)} %constant.19.clone.zi, bf16[2,512,1024]{2,1,0:T(8,128)(2,1)} %constant.20.clone.yf, bf16[2,512,1024]{2,1,0:T(8,128)(2,1)} %constant.21.clone.yi, ...), custom_call_target="tpu_custom_call" | custom-call | tf_op jit(solution)/shard_map/pallas_call | solution.py:229
  71.2 1.7 %copy.12 = f32[64,384]{0,1:T(8,128)} copy(f32[64,384]{1,0:T(8,128)} %shard_map.100) | data formatting | bytes 196608 | tf_op jit(solution)/shard_map/pallas_call | solution.py:229
where the time goes:
time: 73.1 us; the launch traced here: 72.9 us
  Pallas kernels  71.2 us (97%)
  local copies, waits for them, and re-layouts  1.7 us (2%)
    pallas_call x1, Pallas kernels, local(): pl.pallas_call(functools.partial(kernel, points, rows, cols, axes), out_s...  71.2 us
    pallas_call x1, local copies, waits for them, and re-layouts, local(): pl.pallas_call(functools.partial(kernel, points, rows, cols, axes), out_s...  1.7 us

commit v1 on v0

--- a/solution.py
+++ b/solution.py
@@ -62,7 +62,8 @@
     wx = np.broadcast_to(np.repeat(kx, PAD)[None, :], (PAD, lanes))
     wy = np.broadcast_to(np.tile(ky[:, None, None, :], (1, 1, len(kx), 1)).reshape(rows, 1, lanes), (rows, PAD, lanes))
     wz = np.broadcast_to(kz[:, :, None], (cols, PAD, lanes))
-    waves = [np.ascontiguousarray(w).astype(np.float32) for w in (wx, wy, wz)]
+    wt = np.broadcast_to(ky[:, None, :], (rows, px, PAD)).reshape(1, -1)
+    waves = [np.ascontiguousarray(w).astype(np.float32) for w in (wx, wy, wz, wt)]
     return [halves(t) for t in (zf, zi, yf, yi, xf, xi)] + waves
 
 
@@ -99,14 +100,28 @@
     return [a[1] * b[2] - a[2] * b[1], a[2] * b[0] - a[0] * b[2], a[0] * b[1] - a[1] * b[0]]
 
 
-def kernel(points, rows, cols, counts, v_ref, zf, zi, yf, yi, xf, xi, wx, wy, wz, out_ref, *scratch):
+def kernel(points, rows, cols, counts, v_ref, zf, zi, yf, yi, xf, xi, wx, wy, wz, wt, out_ref, *scratch):
     row, col = lax.axis_index("row"), lax.axis_index("col")
     px, py = points // rows, points // cols
     cell, tile = px * py, 2 * px * PAD
     peers = {"row": (row, rows), "col": (col, cols)}
     exchanges = len(counts)
     sends, lands = scratch[:exchanges], scratch[exchanges : 2 * exchanges]
-    send_sems, land_sems = scratch[2 * exchanges : 3 * exchanges], scratch[3 * exchanges :]
+    send_sems, land_sems = scratch[2 * exchanges : 3 * exchanges], scratch[3 * exchanges : 4 * exchanges]
+    held = scratch[4 * exchanges : 4 * exchanges + 4]
+    loads = [
+        pltpu.make_async_copy(source, target, scratch[-1].at[i])
+        for i, (source, target) in enumerate(zip((yf, xf, xi, yi), held))
+    ]
+    for load in loads:
+        load.start()
+    pending = list(range(4))
+
+    def weights(i):
+        if i in pending:
+            pending.remove(i)
+            loads[i].wait()
+        return held[i]
 
     barrier = pltpu.get_barrier_semaphore()
     for axis, (me, n) in peers.items():
@@ -160,13 +175,20 @@
                 for g in got
             ]
             pair.append(jnp.concatenate(stacks, 1))
-        got = swap(at + 1, weave(*turn(*pair, yf, -1)))
-        return turn(*unweave(got), xf, -1)
+        got = swap(at + 1, weave(*turn(*pair, weights(0), -1)))
+        return turn(*unweave(got), weights(1), -1)
 
     def grids(at, re, im):
+        got = swap(at, weave(*turn(re, im, weights(2), 1)))
+        re, im = unweave(got)
+        if re.shape[0] == 5 * PAD:
+            uy, uz = slice(PAD, 2 * PAD), slice(2 * PAD, 3 * PAD)
+            ky, kz = wt[...], wz[col][:, :1]
+            spin_re, spin_im = kz * im[uy] - ky * im[uz], ky * re[uz] - kz * re[uy]
+            re = jnp.concatenate([re[: 3 * PAD], spin_re, re[3 * PAD :]], 0)
+            im = jnp.concatenate([im[: 3 * PAD], spin_im, im[3 * PAD :]], 0)
         n = re.shape[0] // PAD
-        got = swap(at, weave(*turn(re, im, xi, 1)))
-        re, im = turn(*unweave(got), yi, 1)
+        re, im = turn(re, im, weights(3), 1)
         got = swap(at + 1, [
             jnp.concatenate([re[:, q * cell : (q + 1) * cell], im[:, q * cell : (q + 1) * cell]], 1)
             for q in range(cols)])
@@ -190,8 +212,8 @@
     def tendency(at, re, im):
         joined = grids(
             at,
-            jnp.concatenate(re + [-w for w in cross(waves, im)], 0),
-            jnp.concatenate(im + cross(waves, re), 0))
+            jnp.concatenate(re + [-w for w in cross(waves, im)[1:]], 0),
+            jnp.concatenate(im + cross(waves, re)[1:], 0))
         fields = [joined[:, c * cell : (c + 1) * cell] for c in range(6)]
         product = jnp.concatenate(cross(fields[:3], fields[3:]), 1)
         b_re, b_im = spectra(at + 2, dot_left(zf, product))
@@ -221,17 +243,19 @@
         cell, tile = px * py, 2 * px * PAD
         consts = tables(points, rows, cols)
         forward = [(cols, 2 * PAD, 3 * cell), (rows, 3 * PAD, tile)]
-        inverse = lambda n: [(rows, n * PAD, tile), (cols, n * PAD, 2 * cell)]
-        shapes = forward + 2 * (inverse(6) + forward) + inverse(3)
+        inverse = lambda m, n: [(rows, m * PAD, tile), (cols, n * PAD, 2 * cell)]
+        shapes = forward + 2 * (inverse(5, 6) + forward) + inverse(3, 3)
         axes = ["col", "row"] + 2 * ["row", "col", "col", "row"] + ["row", "col"]
         sems = [pltpu.SemaphoreType.DMA(((rows if a == "row" else cols) - 1,)) for a in axes]
+        whole = pl.BlockSpec(memory_space=pltpu.VMEM)
+        held = [pltpu.VMEM(consts[i].shape, jnp.bfloat16) for i in (2, 4, 5, 3)]
         buffers = [pltpu.VMEM(s, jnp.float32) for s in shapes]
         out = pl.pallas_call(
             functools.partial(kernel, points, rows, cols, axes),
             out_shape=jax.ShapeDtypeStruct((points, 3 * cell), jnp.float32),
-            in_specs=[pl.BlockSpec(memory_space=pltpu.VMEM)] * (1 + len(consts)),
+            in_specs=[whole] * 3 + [pl.BlockSpec(memory_space=pl.ANY)] * 4 + [whole] * 4,
             out_specs=pl.BlockSpec(memory_space=pltpu.VMEM),
-            scratch_shapes=buffers + buffers + sems + sems,
+            scratch_shapes=buffers + buffers + sems + sems + held + [pltpu.SemaphoreType.DMA((4,))],
             compiler_params=pltpu.CompilerParams(
                 collective_id=0, has_side_effects=True, vmem_limit_bytes=60 * 1024 * 1024),
         )(velocity.reshape(3 * cell, points), *[jnp.asarray(c) for c in consts])

time: 73.1 us -> 69.9 us (0.956)
  Pallas kernels: 71.2 us -> 68 us
    pallas_call x1, Pallas kernels: 71.2 us -> 68 us  [local(): pl.pallas_call(functools.partial(kernel, points, rows, cols, axes), out_s...]
where the time goes in v1:
time: 69.9 us; the launch traced here: 69.7 us
  Pallas kernels  68 us (97%)
  local copies, waits for them, and re-layouts  1.7 us (2%)
    pallas_call x1, Pallas kernels, local(): pl.pallas_call(functools.partial(kernel, points, rows, cols, axes), out_s...  68 us
    pallas_call x1, local copies, waits for them, and re-layouts, local(): pl.pallas_call(functools.partial(kernel, points, rows, cols, axes), out_s...  1.7 us

profile of v1, /device:TPU:0, one launch (start us, length us, event | category | flops | bytes accessed | tf_op | source)
XLA Modules:
  0.0 69.7 jit_solution(10905728241053504927)
XLA Ops:
  0.0 68.0 %shard_map.109 = f32[64,384]{1,0:T(8,128)} custom-call(f32[384,64]{1,0:T(8,128)} %bitcast.4, bf16[2,64,64]{2,1,0:T(8,128)(2,1)} %constant.20.clone.zf, bf16[2,64,64]{2,1,0:T(8,128)(2,1)} %constant.21.clone.zi, bf16[2,512,1024]{2,1,0:T(8,128)(2,1)} %constant.22.clone.yf, bf16[2,512,1024]{2,1,0:T(8,128)(2,1)} %constant.23.clone.yi, ...), custom_call_target="tpu_custom_call" | custom-call | tf_op jit(solution)/shard_map/pallas_call | solution.py:253
  68.0 1.7 %copy.13 = f32[64,384]{0,1:T(8,128)} copy(f32[64,384]{1,0:T(8,128)} %shard_map.109) | data formatting | bytes 196608 | tf_op jit(solution)/shard_map/pallas_call | solution.py:253
